TPU v7x, 32 devices: a whole 2x2x4 slice. The times are simulated.
32 devices in a mesh: dp: 16 (over z, y, core), mlp: 2 (over x).
Axes of the slice: x: 2, y: 2, z: 4, core: 2. Of those that a mesh axis runs over, the one named last changes fastest.
Arguments:
- block_input: bfloat16 [16, 2, 160, 1024], P('dp', 'mlp'), may hold values from -6 to 6
- span_offset: int32 [16, 2], replicated, may hold values from 0 to 15, as said below
- ln_gain: float32 [1024], replicated, may hold values from 0.5 to 1.5
- ln_bias: float32 [1024], replicated, may hold values from -3 to 3
- w_qkv: bfloat16 [1024, 3072], replicated, may hold values from -0.25 to 0.25
- b_qkv: float32 [3072], replicated, may hold values from -3 to 3
- w_out: bfloat16 [1024, 1024], replicated, may hold values from -1 to 1
- b_out: float32 [1024], replicated, may hold values from -3 to 3
- w_up: bfloat16 [1024, 4096], P(None, 'mlp'), may hold values from -0.1875 to 0.1875
- b_up: float32 [4096], P('mlp'), may hold values from -3 to 3
- w_down: bfloat16 [4096, 1024], P('mlp'), may hold values from -0.09375 to 0.09375
- b_down: float32 [1024], replicated, may hold values from -3 to 3
- cotangent: bfloat16 [16, 2, 160, 1024], P('dp', 'mlp'), may hold values from -6 to 6
Outputs:
- output: bfloat16 [16, 2, 160, 1024], P('dp', 'mlp')
- grad_input: float32 [16, 2, 160, 1024], P('dp', 'mlp')
- grad_ln_gain: float32 [1024], P('mlp')
- grad_ln_bias: float32 [1024], P('mlp')
- grad_w_qkv: float32 [1024, 3072], P(None, 'mlp')
- grad_b_qkv: float32 [3072], P('mlp')
- grad_w_out: float32 [1024, 1024], P(None, 'mlp')
- grad_b_out: float32 [1024], P('mlp')
- grad_w_up: float32 [1024, 4096], P(None, 'mlp')
- grad_b_up: float32 [4096], P('mlp')
- grad_w_down: float32 [4096, 1024], P('mlp')
- grad_b_down: float32 [1024], P('mlp')
Inputs may be any that keep to these rules, and one draw needn't show every extreme that they name: For every sequence s, span_offset[:, s] is a permutation of 0 to 15.
All inputs are finite; a program needn't handle non-finite values.
Results may differ from a plain program's by a relative error of at most 0.02.
Values may be sent and summed in bfloat16 or wider, within the bound.
A program may use at most 256 MiB of HBM per device.

v0:
```python
import math
import jax
import jax.numpy as jnp
from jax import lax
from jax.sharding import PartitionSpec as P

HEADS = 16
HEAD_DIM = 64
ROT = 16
EPSILON = 1e-05
ROPE_BASE = 10000.0
SQRT_HALF = 1.0 / math.sqrt(2.0)
INV_ROOT_TWO_PI = 1.0 / math.sqrt(2.0 * math.pi)


def rotate(values, positions, sign_factor):
    half_rot = ROT // 2
    frequency = ROPE_BASE ** (-(jnp.arange(half_rot, dtype=jnp.float32) * 2.0 / ROT))
    angles = positions.astype(jnp.float32)[:, None] * frequency[None, :]
    cosine = jnp.cos(angles)[:, None, :]
    sine_part = sign_factor * jnp.sin(angles)[:, None, :]
    first_half = values[..., :half_rot]
    second_half = values[..., half_rot:ROT]
    return jnp.concatenate(
        [
            first_half * cosine - second_half * sine_part,
            second_half * cosine + first_half * sine_part,
            values[..., ROT:],
        ],
        axis=-1,
    )


def gelu_exact(values):
    return 0.5 * values * (1.0 + lax.erf(values * SQRT_HALF))


def gelu_slope(values):
    return (
        0.5 * (1.0 + lax.erf(values * SQRT_HALF))
        + values * jnp.exp(-0.5 * values * values) * INV_ROOT_TWO_PI
    )


def piece_count(total_rows):
    count_blocks = max(1, total_rows // 1024)
    while total_rows % count_blocks:
        count_blocks += 1
    return count_blocks


def row_positions(offsets, count_rows, tok_count):
    index_all = jnp.arange(count_rows, dtype=jnp.int32)
    span_of = index_all // tok_count
    within = index_all - span_of * tok_count
    matches = span_of[:, None] == jnp.arange(offsets.shape[0], dtype=jnp.int32)[None, :]
    offset_of = jnp.sum(jnp.where(matches, offsets[None, :], 0), axis=1)
    return offset_of * tok_count + within


def contract_rows(left_mat, right_mat):
    return lax.dot_general(
        left_mat, right_mat, (((0,), (0,)), ((), ())), preferred_element_type=jnp.float32
    )


def contract_cols(left_mat, right_mat):
    return lax.dot_general(
        left_mat, right_mat, (((1,), (1,)), ((), ())), preferred_element_type=jnp.float32
    )


def local(
    block_input,
    span_offset,
    ln_gain,
    ln_bias,
    w_qkv,
    b_qkv,
    w_out,
    b_out,
    w_up,
    b_up,
    w_down,
    b_down,
    cotangent,
):
    tok_count = block_input.shape[2]
    model_width = block_input.shape[3]
    scale_dot = 1.0 / math.sqrt(HEAD_DIM)
    span_here = lax.axis_index("dp")
    seq_here = lax.axis_index("mlp")
    offsets = lax.dynamic_index_in_dim(span_offset, seq_here, axis=1, keepdims=False)
    offset_here = lax.dynamic_index_in_dim(offsets, span_here, axis=0, keepdims=False)
    positions = offset_here * tok_count + jnp.arange(tok_count, dtype=jnp.int32)
    row_data = block_input[0, 0].astype(jnp.float32)
    centre = jnp.mean(row_data, axis=-1, keepdims=True)
    centred = row_data - centre
    spread = jnp.mean(centred * centred, axis=-1, keepdims=True)
    inv_scale = lax.rsqrt(spread + EPSILON)
    unit_rows = centred * inv_scale
    normed = (unit_rows * ln_gain + ln_bias).astype(jnp.bfloat16)
    project = jnp.dot(normed, w_qkv, preferred_element_type=jnp.float32) + b_qkv
    queries = rotate(
        project[:, :model_width].reshape(tok_count, HEADS, HEAD_DIM), positions, 1.0
    ).astype(jnp.bfloat16)
    keys_here = rotate(
        project[:, model_width : 2 * model_width].reshape(tok_count, HEADS, HEAD_DIM),
        positions,
        1.0,
    ).astype(jnp.bfloat16)
    values_here = (
        project[:, 2 * model_width :].reshape(tok_count, HEADS, HEAD_DIM).astype(jnp.bfloat16)
    )
    keys_flat = keys_here.reshape(tok_count, model_width)
    values_flat = values_here.reshape(tok_count, model_width)
    start_state = (
        jnp.zeros((tok_count, HEADS, HEAD_DIM), jnp.float32),
        jnp.zeros((HEADS, tok_count), jnp.float32),
    )
    keys_piece = lax.all_gather(keys_flat, "dp", axis=0, tiled=True)
    values_piece = lax.all_gather(values_flat, "dp", axis=0, tiled=True)
    piece_rows = keys_piece.shape[0]
    blocks = piece_count(piece_rows)
    sub_rows = piece_rows // blocks
    key_pos = row_positions(offsets, piece_rows, tok_count)

    def attend_one_block(state_now, packed):
        keys_blk, values_blk, pos_blk = packed
        key_heads = keys_blk.reshape(sub_rows, HEADS, HEAD_DIM)
        value_heads = values_blk.reshape(sub_rows, HEADS, HEAD_DIM)
        scores = (
            jnp.einsum("qhd,khd->hqk", queries, key_heads, preferred_element_type=jnp.float32)
            * scale_dot
        )
        allowed = pos_blk[None, :] <= positions[:, None]
        weights_exp = jnp.where(allowed[None], jnp.exp(scores), 0.0)
        mixed_sum, totals = state_now
        mixed_sum = mixed_sum + jnp.einsum(
            "hqk,khd->qhd",
            weights_exp.astype(jnp.bfloat16),
            value_heads,
            preferred_element_type=jnp.float32,
        )
        return ((mixed_sum, totals + jnp.sum(weights_exp, axis=-1)), None)

    state_now, _unused = lax.scan(
        attend_one_block,
        start_state,
        (
            keys_piece.reshape(blocks, sub_rows, model_width),
            values_piece.reshape(blocks, sub_rows, model_width),
            key_pos.reshape(blocks, sub_rows),
        ),
    )
    mixed_sum, totals = state_now
    attended = mixed_sum / totals.T[:, :, None]
    attended_low = attended.reshape(tok_count, model_width).astype(jnp.bfloat16)
    attn_branch = jnp.dot(attended_low, w_out, preferred_element_type=jnp.float32) + b_out
    normed_all = lax.all_gather(normed, "mlp", axis=0, tiled=True)
    up_proj = jnp.dot(normed_all, w_up, preferred_element_type=jnp.float32) + b_up
    activated = gelu_exact(up_proj).astype(jnp.bfloat16)
    mlp_branch = (
        lax.psum_scatter(
            jnp.dot(activated, w_down, preferred_element_type=jnp.float32).astype(jnp.bfloat16),
            "mlp",
            scatter_dimension=0,
            tiled=True,
        ).astype(jnp.float32)
        + b_down
    )
    output = (row_data + attn_branch + mlp_branch).astype(jnp.bfloat16)
    grad_out = cotangent[0, 0]
    grad_w_out = contract_rows(attended_low, grad_out)
    grad_bias_out = jnp.sum(grad_out.astype(jnp.float32), axis=0)
    grad_all = lax.all_gather(grad_out, "mlp", axis=0, tiled=True)
    grad_w_down = contract_rows(activated, grad_all)
    grad_act = contract_cols(grad_all, w_down)
    grad_up = (grad_act * gelu_slope(up_proj)).astype(jnp.bfloat16)
    grad_w_up = contract_rows(normed_all, grad_up)
    grad_b_up = jnp.sum(grad_up.astype(jnp.float32), axis=0)
    grad_norm_mlp = lax.psum_scatter(
        contract_cols(grad_up, w_up).astype(jnp.bfloat16), "mlp", scatter_dimension=0, tiled=True
    ).astype(jnp.float32)
    grad_att = contract_cols(grad_out, w_out).reshape(tok_count, HEADS, HEAD_DIM)
    grad_mixed = (grad_att / totals.T[:, :, None]).astype(jnp.bfloat16)
    grad_totals = ((-jnp.sum(grad_att * attended, axis=-1)).T / totals).astype(jnp.bfloat16)
    grad_totals_wide = grad_totals.astype(jnp.float32)[:, :, None]
    zero_heads = jnp.zeros((tok_count, HEADS, HEAD_DIM), jnp.float32)
    grad_query_sum = zero_heads
    keys_piece = lax.all_gather(keys_flat, "dp", axis=0, tiled=True)
    values_piece = lax.all_gather(values_flat, "dp", axis=0, tiled=True)
    piece_rows = keys_piece.shape[0]
    blocks = piece_count(piece_rows)
    back_sub_rows = piece_rows // blocks
    key_pos = row_positions(offsets, piece_rows, tok_count)

    def back_one_block(running_sum, packed):
        keys_blk, values_blk, pos_blk = packed
        key_heads = keys_blk.reshape(back_sub_rows, HEADS, HEAD_DIM)
        value_heads = values_blk.reshape(back_sub_rows, HEADS, HEAD_DIM)
        scores = (
            jnp.einsum("qhd,khd->hqk", queries, key_heads, preferred_element_type=jnp.float32)
            * scale_dot
        )
        allowed = pos_blk[None, :] <= positions[:, None]
        weights_exp = jnp.where(allowed[None], jnp.exp(scores), 0.0)
        grad_exp = jnp.einsum(
            "qhd,khd->hqk", grad_mixed, value_heads, preferred_element_type=jnp.float32
        )
        grad_scores = (weights_exp * (grad_exp + grad_totals_wide)).astype(jnp.bfloat16)
        running_sum = running_sum + scale_dot * jnp.einsum(
            "hqk,khd->qhd", grad_scores, key_heads, preferred_element_type=jnp.float32
        )
        grad_key_blk = scale_dot * jnp.einsum(
            "hqk,qhd->khd", grad_scores, queries, preferred_element_type=jnp.float32
        )
        grad_value_blk = jnp.einsum(
            "hqk,qhd->khd",
            weights_exp.astype(jnp.bfloat16),
            grad_mixed,
            preferred_element_type=jnp.float32,
        )
        joined = jnp.concatenate(
            [
                grad_key_blk.reshape(back_sub_rows, model_width),
                grad_value_blk.reshape(back_sub_rows, model_width),
            ],
            axis=1,
        )
        return (running_sum, joined)

    grad_query_sum, stacked = lax.scan(
        back_one_block,
        grad_query_sum,
        (
            keys_piece.reshape(blocks, back_sub_rows, model_width),
            values_piece.reshape(blocks, back_sub_rows, model_width),
            key_pos.reshape(blocks, back_sub_rows),
        ),
    )
    grad_kv_sum = stacked.reshape(piece_rows, 2 * model_width)
    grad_kv = lax.psum_scatter(
        grad_kv_sum.astype(jnp.bfloat16), "dp", scatter_dimension=0, tiled=True
    ).astype(jnp.float32)
    grad_keys = grad_kv[:, :model_width].reshape(tok_count, HEADS, HEAD_DIM)
    grad_values = grad_kv[:, model_width:].reshape(tok_count, HEADS, HEAD_DIM)
    grad_query_pre = rotate(grad_query_sum, positions, -1.0).reshape(tok_count, model_width)
    grad_key_pre = rotate(grad_keys, positions, -1.0).reshape(tok_count, model_width)
    grad_project = jnp.concatenate(
        [grad_query_pre, grad_key_pre, grad_values.reshape(tok_count, model_width)], axis=1
    ).astype(jnp.bfloat16)
    grad_w_qkv = contract_rows(normed, grad_project)
    grad_b_qkv = jnp.sum(grad_project.astype(jnp.float32), axis=0)
    grad_normed = contract_cols(grad_project, w_qkv) + grad_norm_mlp
    grad_ln_gain = jnp.sum(grad_normed * unit_rows, axis=0)
    grad_ln_bias = jnp.sum(grad_normed, axis=0)
    grad_unit = grad_normed * ln_gain
    grad_rows = inv_scale * (
        grad_unit
        - jnp.mean(grad_unit, axis=-1, keepdims=True)
        - unit_rows * jnp.mean(grad_unit * unit_rows, axis=-1, keepdims=True)
    )
    grad_input = (grad_out.astype(jnp.float32) + grad_rows).reshape(1, 1, tok_count, model_width)
    part_qkv, part_out, part_bqkv, part_bias, part_gain, part_shift = (
        lax.psum_scatter(
            grad_w_qkv.astype(jnp.bfloat16), "mlp", scatter_dimension=1, tiled=True
        ).astype(jnp.float32),
        lax.psum_scatter(
            grad_w_out.astype(jnp.bfloat16), "mlp", scatter_dimension=1, tiled=True
        ).astype(jnp.float32),
        lax.psum_scatter(
            grad_b_qkv.astype(jnp.bfloat16), "mlp", scatter_dimension=0, tiled=True
        ).astype(jnp.float32),
        lax.psum_scatter(
            grad_bias_out.astype(jnp.bfloat16), "mlp", scatter_dimension=0, tiled=True
        ).astype(jnp.float32),
        lax.psum_scatter(
            grad_ln_gain.astype(jnp.bfloat16), "mlp", scatter_dimension=0, tiled=True
        ).astype(jnp.float32),
        lax.psum_scatter(
            grad_ln_bias.astype(jnp.bfloat16), "mlp", scatter_dimension=0, tiled=True
        ).astype(jnp.float32),
    )
    summed = (
        lax.psum(part_qkv.astype(jnp.bfloat16), "dp").astype(jnp.float32),
        lax.psum(part_out.astype(jnp.bfloat16), "dp").astype(jnp.float32),
        lax.psum(part_bqkv.astype(jnp.bfloat16), "dp").astype(jnp.float32),
        lax.psum(part_bias.astype(jnp.bfloat16), "dp").astype(jnp.float32),
        lax.psum(part_gain.astype(jnp.bfloat16), "dp").astype(jnp.float32),
        lax.psum(part_shift.astype(jnp.bfloat16), "dp").astype(jnp.float32),
        lax.psum(grad_w_up.astype(jnp.bfloat16), "dp").astype(jnp.float32),
        lax.psum(grad_b_up.astype(jnp.bfloat16), "dp").astype(jnp.float32),
        lax.psum(grad_w_down.astype(jnp.bfloat16), "dp").astype(jnp.float32),
    )
    return (
        output.reshape(1, 1, tok_count, model_width),
        grad_input,
        summed[4],
        summed[5],
        summed[0],
        summed[2],
        summed[1],
        summed[3],
        summed[6],
        summed[7],
        summed[8],
        summed[3],
    )


def solution(mesh):
    return jax.shard_map(
        local,
        mesh=mesh,
        in_specs=(
            P("dp", "mlp", None, None),
            P(),
            P(),
            P(),
            P(),
            P(),
            P(),
            P(),
            P(None, "mlp"),
            P("mlp"),
            P("mlp", None),
            P(),
            P("dp", "mlp", None, None),
        ),
        out_specs=(
            P("dp", "mlp", None, None),
            P("dp", "mlp", None, None),
            P("mlp"),
            P("mlp"),
            P(None, "mlp"),
            P("mlp"),
            P(None, "mlp"),
            P("mlp"),
            P(None, "mlp"),
            P("mlp"),
            P("mlp", None),
            P("mlp"),
        ),
        check_vma=False,
    )
```

profile of v0, /device:TPU:0, one launch (start us, length us, event | category | flops | bytes accessed | tf_op | source)
XLA Modules:
  0.0 848.6 jit_solution(7495591158141131622)
XLA Ops:
  38.3 52.1 %all-gather.6.cloned.1.call-done = bf16[2560,1024]{1,0:T(8,128)(2,1)} async-done(((bf16[160,1024]{1,0:T(8,128)(2,1)}), bf16[2560,1024]{1,0:T(8,128)(2,1)}) %all-gather.6.cloned.1.call-update) | async-done | bytes 5242896 | tf_op jit(solution)/shard_map/all_gather | solution.py:121
  90.4 7.9 copy.85
  98.3 49.4 %all-gather.4.cloned.1.call-done = bf16[2560,1024]{1,0:T(8,128)(2,1)} async-done(((bf16[160,1024]{1,0:T(8,128)(2,1)}), bf16[2560,1024]{1,0:T(8,128)(2,1)}) %all-gather.4.cloned.1.call-update) | async-done | bytes 5242896 | tf_op jit(solution)/shard_map/all_gather | solution.py:122
  147.7 7.9 copy.84
  155.5 40.2 %while.26 = (s32[]{:T(128)}, f32[160,16,64]{0,2,1:T(8,128)}, f32[16,160]{1,0:T(8,128)S(1)}, bf16[2,1280,1024]{1,2,0:T(8,128)(2,1)}, s32[2,1280]{1,0:T(2,128)S(1)...) while((s32[]{:T(128)}, f32[160,16,64]{0,2,1:T(8,128)}, ...), condition=%wide.region_5.6_spmd.clone, body=%wide.region_3.5_spmd.clone.sunk | while | flops 859056768 | bytes 44253560 | solution.py:147
  160.1 6.5 fusion.124
  166.7 8.9 %fusion.125 = f32[160,16,64]{0,2,1:T(8,128)} fusion(bf16[1280,16,64]{0,2,1:T(8,128)(2,1)} %bitcast.209, f32[16,1280,160]{1,2,0:T(8,128)} %get-tuple-element.480, pred[160,1280]{1,0:T(8,128)(4,1)S(1)} %broadcast_compare_fusion.4, f32[160,16,64]{0,2,1:T(8,128)} %get-tuple-element.505, pred[]{:T(512)S(6)} %compare.6), kind=kOutput, calls=%fused_computation.10.clone.1 | convolution fusion | flops 429588480 | bytes 17244160 | tf_op jit(solution)/shard_map/while/body/eval_jaxpr/hqk,khd->qhd/dot_general | solution.py:139
  180.1 6.5 fusion.124
  186.7 9.1 %fusion.125 = f32[160,16,64]{0,2,1:T(8,128)} fusion(bf16[1280,16,64]{0,2,1:T(8,128)(2,1)} %bitcast.209, f32[16,1280,160]{1,2,0:T(8,128)} %get-tuple-element.480, pred[160,1280]{1,0:T(8,128)(4,1)S(1)} %broadcast_compare_fusion.4, f32[160,16,64]{0,2,1:T(8,128)} %get-tuple-element.505, pred[]{:T(512)S(6)} %compare.6), kind=kOutput, calls=%fused_computation.10.clone.1 | convolution fusion | flops 429588480 | bytes 17244160 | tf_op jit(solution)/shard_map/while/body/eval_jaxpr/hqk,khd->qhd/dot_general | solution.py:139
  198.7 110.8 %while.27 = (s32[]{:T(128)}, f32[160,16,64]{0,2,1:T(8,128)}, bf16[2,1280,2048]{2,1,0:T(8,128)(2,1)}, bf16[2,1280,1024]{1,2,0:T(8,128)(2,1)}, s32[2,1280]{1,0:T(2...) while((s32[]{:T(128)}, f32[160,16,64]{0,2,1:T(8,128)}, ...), condition=%wide.region_9.10_spmd.clone, body=%wide.region_8.9_spmd.clone.sunk | while | flops 2137170048 | bytes 206425072 | solution.py:233
  203.2 6.6 fusion.136
  210.1 9.9 %fusion.137 = bf16[16,160,1280]{2,1,0:T(8,128)(2,1)S(1)} fusion(f32[16,1280,160]{1,2,0:T(8,128)} %fusion.136, bf16[1280,16,64]{0,2,1:T(8,128)(2,1)} %bitcast.211, bf16[160,16,64]{0,2,1:T(8,128)(2,1)} %get-tuple-element.555, f32[16,160]{1,0:T(8,128)S(1)} %bitcast.219, pred[160,1280]{1,0:T(8,128)(4,1)S(1)} %broadcast_compare_fusion.5), kind=kOutput, calls=%fused_computation.20.clone.1 | convolution fusion | flops 435814400 | bytes 22824960 | tf_op jit(solution)/shard_map/while/body/eval_jaxpr/qhd,khd->hqk/dot_general | solution.py:208
  233.6 8.0 copy.108
  247.1 6.9 fusion.138
  258.4 6.6 fusion.136
  265.2 9.9 %fusion.137 = bf16[16,160,1280]{2,1,0:T(8,128)(2,1)S(1)} fusion(f32[16,1280,160]{1,2,0:T(8,128)} %fusion.136, bf16[1280,16,64]{0,2,1:T(8,128)(2,1)} %bitcast.211, bf16[160,16,64]{0,2,1:T(8,128)(2,1)} %get-tuple-element.555, f32[16,160]{1,0:T(8,128)S(1)} %bitcast.219, pred[160,1280]{1,0:T(8,128)(4,1)S(1)} %broadcast_compare_fusion.5), kind=kOutput, calls=%fused_computation.20.clone.1 | convolution fusion | flops 435814400 | bytes 22824960 | tf_op jit(solution)/shard_map/while/body/eval_jaxpr/qhd,khd->hqk/dot_general | solution.py:208
  288.7 8.0 copy.108
  302.4 7.1 fusion.138
  326.5 101.3 %reduce-scatter.8.cloned.1.call-done = bf16[160,2048]{1,0:T(8,128)(2,1)} async-done(((bf16[2560,2048]{1,0:T(8,128)(2,1)}), bf16[160,2048]{1,0:T(8,128)(2,1)}) %reduce-scatter.8.cloned.1.call-update) | async-done | bytes 655376 | tf_op jit(solution)/shard_map/reduce_scatter | solution.py:243
  442.0 17.8 %all_gather.16 = bf16[320,1024]{1,0:T(8,128)(2,1)S(1)} all-gather(bf16[160,1024]{1,0:T(8,128)(2,1)S(1)} %copy-done.8), channel_id=1, replica_groups=mesh['dp'=16,'mlp'=2] {'mlp'}, dimensions={0}, use_global_device_ids=true | all-gather | bytes 983040 | tf_op jit(solution)/shard_map/all_gather | solution.py:160
  459.8 5.7 multiply_convert_fusion
  469.1 9.4 %all-gather = bf16[1,1,320,1024]{3,2,1,0:T(8,128)(2,1)S(1)} all-gather(bf16[1,1,160,1024]{3,2,1,0:T(8,128)(2,1)S(1)} %copy-done.11), channel_id=2, replica_groups=mesh['dp'=16,'mlp'=2] {'mlp'}, dimensions={2}, use_global_device_ids=true | all-gather | bytes 983040 | tf_op jit(solution)/shard_map/all_gather | solution.py:176
  478.5 6.4 fusion.68
  488.6 6.1 convolution_convert_fusion.2
  499.1 49.8 %reduce-scatter.12.cloned.1.call-done = bf16[1024,1536]{1,0:T(8,128)(2,1)} async-done(((bf16[1024,3072]{1,0:T(8,128)(2,1)}), bf16[1024,1536]{1,0:T(8,128)(2,1)}) %reduce-scatter.12.cloned.1.call-update) | async-done | bytes 3145744 | tf_op jit(solution)/shard_map/reduce_scatter | solution.py:266
  551.5 16.2 %reduce-scatter.6.cloned.1.call-done = bf16[160,1024]{1,0:T(8,128)(2,1)} async-done(((bf16[320,1024]{1,0:T(8,128)(2,1)}), bf16[160,1024]{1,0:T(8,128)(2,1)}) %reduce-scatter.6.cloned.1.call-update) | async-done | bytes 327696 | tf_op jit(solution)/shard_map/reduce_scatter | solution.py:164
  570.4 15.7 %reduce-scatter.10.cloned.1.call-done = bf16[160,1024]{1,0:T(8,128)(2,1)} async-done(((bf16[320,1024]{1,0:T(8,128)(2,1)}), bf16[160,1024]{1,0:T(8,128)(2,1)}) %reduce-scatter.10.cloned.1.call-update) | async-done | bytes 327696 | tf_op jit(solution)/shard_map/reduce_scatter | solution.py:182
  586.1 6.1 fusion.53
  592.2 6.9 all-reduce.6
  599.4 63.3 %all-reduce.4 = (bf16[512]{0:T(512)(128)(2,1)S(1)}, bf16[512]{0:T(512)(128)(2,1)S(1)}, bf16[1536]{0:T(1024)(128)(2,1)S(1)}, bf16[512]{0:T(512)(128)(2,1)S(1)}, bf16[2048]{0:T(1024)(128)(2,1)S(1)}) all-reduce(bf16[512]{0:T(512)(128)(2,1)S(1)} %dynamic-slice.2, ...), channel_id=1, replica_groups=mesh['dp'=16,'mlp'=2] {'dp'}, use_global_device_ids=true, to_apply=%region_16.17 | all-reduce | flops 5120 | bytes 20480 | tf_op jit(solution)/shard_map/psum | solution.py:290
  667.2 157.0 %all-reduce.9.cloned.1.call-done = (bf16[1024,1536]{1,0:T(8,128)(2,1)}, bf16[1024,512]{1,0:T(8,128)(2,1)}, bf16[1024,2048]{1,0:T(8,128)(2,1)}, bf16[2048,1024]{1,0:T(8,128)(2,1)}) async-done(((bf16[1024,1536]{1,0:T(8,128)(2,1)}, bf16[1024,512]{1,0:T(8,128)(2,1)}, bf16[1024,2048]{1,0:T(8,128)(2,1)}, bf16[2048,1024]{1,0:T(8,128)(2,1)}), (bf16[1024,1536]{1,0:T(8,128)(2,1)}, bf16[1024,512]{1,0:T(8,128)(2,1)}, ...) | async-done | bytes 12582928 | tf_op jit(solution)/shard_map/psum | solution.py:286
  824.2 6.8 convert_element_type.175
  (203 shorter events, 151.4 us)
Async XLA Ops:
  7.2 188.6 %copy-start = (bf16[1024,1024]{1,0:T(8,128)(2,1)S(1)}, bf16[1024,1024]{1,0:T(8,128)(2,1)}, u32[]{:S(2)}) copy-start(bf16[1024,1024]{1,0:T(8,128)(2,1)} %param.23) | copy-start | bytes 6291460
  7.2 83.2 %all-gather.6.cloned.1.call-start = ((), (), s32[]{:S(2)}) async-start(), calls=%async_computation.6 | async-start | bytes 5570560 | tf_op jit(solution)/shard_map/all_gather | solution.py:121
  10.2 15.1 %copy-start.17 = (f32[160,8]{1,0:T(8,128)}, f32[160,8]{1,0:T(8,128)S(1)}, u32[]{:S(2)}) copy-start(f32[160,8]{1,0:T(8,128)S(1)} %copy.82) | copy-start | bytes 15364
  31.8 115.8 %all-gather.4.cloned.1.call-start = ((), (), s32[]{:S(2)}) async-start(), calls=%async_computation.5 | async-start | bytes 5570560 | tf_op jit(solution)/shard_map/all_gather | solution.py:122
  33.8 394.0 %reduce-scatter.8.cloned.1.call-start = ((), (), s32[]{:S(2)}) async-start(), calls=%async_computation.8 | async-start | bytes 11141120 | tf_op jit(solution)/shard_map/reduce_scatter | solution.py:243
  155.5 40.2 %copy-start.10 = (bf16[1,1,160,1024]{3,2,1,0:T(8,128)(2,1)S(1)}, bf16[1,1,160,1024]{3,2,1,0:T(8,128)(2,1)}, u32[]{:S(2)}) copy-start(bf16[1,1,160,1024]{3,2,1,0:T(8,128)(2,1)} %param.29) | copy-start | bytes 983044
  203.2 6.6 copy-start.3
  220.1 7.1 copy-start.2
  258.4 6.6 copy-start.3
  275.2 7.1 copy-start.2
  309.5 5.7 copy-start.4
  309.5 189.6 %reduce-scatter.14.cloned.1.call-start = ((), (), s32[]{:S(2)}) async-start(), calls=%async_computation.11 | async-start | bytes 3145728 | tf_op jit(solution)/shard_map/reduce_scatter | solution.py:269
  313.5 235.4 %reduce-scatter.12.cloned.1.call-start = ((), (), s32[]{:S(2)}) async-start(), calls=%async_computation.10 | async-start | bytes 9437184 | tf_op jit(solution)/shard_map/reduce_scatter | solution.py:266
  317.7 6.9 copy-start.16
  441.9 17.9 %copy-start.35 = (f32[2048]{0:T(1024)S(1)}, f32[2048]{0:T(1024)}, u32[]{:S(2)}) copy-start(f32[2048]{0:T(1024)} %param.26) | copy-start | bytes 24580
  441.9 125.8 %reduce-scatter.6.cloned.1.call-start = ((), (), s32[]{:S(2)}) async-start(), calls=%async_computation.7 | async-start | bytes 983040 | tf_op jit(solution)/shard_map/reduce_scatter | solution.py:164
  459.8 5.7 copy-start.21
  459.8 6.8 copy-start.33
  469.1 117.0 %reduce-scatter.10.cloned.1.call-start = ((), (), s32[]{:S(2)}) async-start(), calls=%async_computation.9 | async-start | bytes 983040 | tf_op jit(solution)/shard_map/reduce_scatter | solution.py:182
  478.5 6.5 copy-start.22
  478.5 7.5 copy-start.34
  488.5 335.7 %all-reduce.9.cloned.1.call-start = ((), (), s32[]{:S(2)}) async-start(), calls=%async_computation.12 | async-start | bytes 25165824 | tf_op jit(solution)/shard_map/psum | solution.py:286
  488.6 6.1 copy-start.23
  488.6 6.1 copy-start.38
  548.9 18.8 %copy-start.6 = (bf16[1,1,160,1024]{3,2,1,0:T(8,128)(2,1)S(1)}, bf16[1,1,160,1024]{3,2,1,0:T(8,128)(2,1)}, u32[]{:S(2)}) copy-start(bf16[1,1,160,1024]{3,2,1,0:T(8,128)(2,1)} %param.17) | copy-start | bytes 983044
  548.9 18.8 %copy-start.24 = (f32[1024]{0:T(1024)S(1)}, f32[1024]{0:T(1024)}, u32[]{:S(2)}) copy-start(f32[1024]{0:T(1024)} %param.28) | copy-start | bytes 12292
  548.9 18.8 %copy-start.25 = (f32[1024]{0:T(1024)S(1)}, f32[1024]{0:T(1024)}, u32[]{:S(2)}) copy-start(f32[1024]{0:T(1024)} %param.24) | copy-start | bytes 12292
  549.0 37.1 %copy-start.27 = (f32[160]{0:T(256)S(1)}, f32[160]{0:T(256)}, u32[]{:S(2)}) copy-start(f32[160]{0:T(256)} %copy-done.26) | copy-start | bytes 1924
  549.0 37.1 %copy-start.28 = (f32[1024]{0:T(1024)S(1)}, f32[1024]{0:T(1024)}, u32[]{:S(2)}) copy-start(f32[1024]{0:T(1024)} %param.19) | copy-start | bytes 12292
  549.0 37.1 %copy-start.30 = (f32[160]{0:T(256)S(1)}, f32[160]{0:T(256)}, u32[]{:S(2)}) copy-start(f32[160]{0:T(256)} %copy-done.29) | copy-start | bytes 1924
  663.9 176.8 %copy-start.31 = (f32[512]{0:T(512)}, f32[512]{0:T(512)S(1)}, u32[]{:S(2)}) copy-start(f32[512]{0:T(512)S(1)} %convert_element_type.173) | copy-start | bytes 6148
  824.2 6.8 copy-start.12
  (19 other events, 47.1 us)
Sparse Core Ops, SparseCore 0:
  31.9 58.4 all-gather.5
  93.3 54.3 all-gather.3
  309.6 118.0 reduce-scatter.7
  430.4 38.5 reduce-scatter.13
  471.8 77.1 reduce-scatter.11
  551.6 16.0 reduce-scatter.5
  570.0 16.0 reduce-scatter.9
  591.2 232.9 all-reduce.8
where the time goes:
time: 855 us; the launch traced here: 849 us
  waiting for transfers between devices  442 us (52%)
  matrix products  139 us (16%)
  local copies, waits for them, and re-layouts  107 us (13%)
  blocking collectives  97.4 us (11%)
  other arithmetic  44.8 us (5%)
  between operations  17 us (2%)
    psum x1, waiting for transfers between devices, local(): lax.psum(part_qkv.astype(jnp.bfloat16), 'dp').astype(jnp.float32)  157 us
    reduce_scatter x1, waiting for transfers between devices, local(): lax.psum_scatter(grad_kv_sum.astype(jnp.bfloat16), 'dp', scatter_dimensio...  101 us
    psum x1, blocking collectives, local(): lax.psum(part_gain.astype(jnp.bfloat16), 'dp').astype(jnp.float32)  63.3 us
    all_gather x1, waiting for transfers between devices, local(): keys_piece = lax.all_gather(keys_flat, 'dp', axis=0, tiled=True)  52.1 us
    reduce_scatter x1, waiting for transfers between devices, local(): lax.psum_scatter(grad_w_qkv.astype(jnp.bfloat16), 'mlp', scatter_dimensio...  49.8 us
    all_gather x1, waiting for transfers between devices, local(): values_piece = lax.all_gather(values_flat, 'dp', axis=0, tiled=True)  49.4 us
    dynamic_update_slice x4, local copies, waits for them, and re-layouts, local(): lax.scan(back_one_block, grad_query_sum, (keys_piece.reshape(blocks, back...  27.2 us
    unnamed x83, local copies, waits for them, and re-layouts  23 us
  transfers between devices with their start and end apart: 8, of which 7 were waited for; matrix products, arithmetic and copies ran while one was open for 10% of the time, Pallas kernels for 0%

commit v1 on v0

--- a/solution.py
+++ b/solution.py
@@ -118,8 +118,11 @@
         jnp.zeros((tok_count, HEADS, HEAD_DIM), jnp.float32),
         jnp.zeros((HEADS, tok_count), jnp.float32),
     )
-    keys_piece = lax.all_gather(keys_flat, "dp", axis=0, tiled=True)
-    values_piece = lax.all_gather(values_flat, "dp", axis=0, tiled=True)
+    keys_piece, values_piece = jnp.split(
+        lax.all_gather(jnp.concatenate([keys_flat, values_flat], axis=1), "dp", axis=0, tiled=True),
+        [keys_flat.shape[1]],
+        axis=1,
+    )
     piece_rows = keys_piece.shape[0]
     blocks = piece_count(piece_rows)
     sub_rows = piece_rows // blocks

time: 855 us -> 915 us (1.070)
  local copies, waits for them, and re-layouts: 107 us -> 129 us
  waiting for transfers between devices: 442 us -> 461 us
  matrix products: 139 us -> 157 us
    all_gather x0 -> x1, waiting for transfers between devices: none -> 84.7 us  [local(): lax.all_gather(jnp.concatenate([keys_flat, values_flat], axis=1), 'dp', a...]
    all_gather x1, waiting for transfers between devices: 52.1 us -> 0.02 us  [local(): keys_piece = lax.all_gather(keys_flat, 'dp', axis=0, tiled=True)]
    dynamic_slice x8 -> x16, local copies, waits for them, and re-layouts: 17.6 us -> 57.1 us  [local(): lax.scan(attend_one_block, start_state, (keys_piece.reshape(blocks, sub_r...]
    unnamed x83 -> x79, local copies, waits for them, and re-layouts: 23 us -> 6.82 us
    all_gather x1, waiting for transfers between devices: 49.4 us -> 34.3 us  [local(): values_piece = lax.all_gather(values_flat, 'dp', axis=0, tiled=True)]
    split x0 -> x1, local copies, waits for them, and re-layouts: none -> 9.39 us  [local(): jnp.split(lax.all_gather(jnp.concatenate([keys_flat, values_flat], axis=1...]
  transfers between devices with their start and end apart: 8 -> 9, of which waited for: 7 -> 7; matrix products, arithmetic and copies ran while one was open for 10% -> 17% of each run, Pallas kernels for 0% -> 0%
where the time goes in v1:
time: 915 us; the launch traced here: 909 us
  waiting for transfers between devices  461 us (50%)
  matrix products  157 us (17%)
  local copies, waits for them, and re-layouts  129 us (14%)
  blocking collectives  97.1 us (11%)
  other arithmetic  46.8 us (5%)
  between operations  16.5 us (2%)
    psum x1, waiting for transfers between devices, local(): lax.psum(part_qkv.astype(jnp.bfloat16), 'dp').astype(jnp.float32)  157 us
    reduce_scatter x1, waiting for transfers between devices, local(): lax.psum_scatter(grad_kv_sum.astype(jnp.bfloat16), 'dp', scatter_dimensio...  101 us
    all_gather x1, waiting for transfers between devices, local(): lax.all_gather(jnp.concatenate([keys_flat, values_flat], axis=1), 'dp', a...  84.7 us
    psum x1, blocking collectives, local(): lax.psum(part_gain.astype(jnp.bfloat16), 'dp').astype(jnp.float32)  63.1 us
    dynamic_slice x16, local copies, waits for them, and re-layouts, local(): lax.scan(attend_one_block, start_state, (keys_piece.reshape(blocks, sub_r...  57.1 us
    reduce_scatter x1, waiting for transfers between devices, local(): lax.psum_scatter(grad_w_qkv.astype(jnp.bfloat16), 'mlp', scatter_dimensio...  49.8 us
    all_gather x1, waiting for transfers between devices, local(): values_piece = lax.all_gather(values_flat, 'dp', axis=0, tiled=True)  34.3 us
    dynamic_update_slice x4, local copies, waits for them, and re-layouts, local(): lax.scan(back_one_block, grad_query_sum, (keys_piece.reshape(blocks, back...  27.1 us
  transfers between devices with their start and end apart: 9, of which 7 were waited for; matrix products, arithmetic and copies ran while one was open for 17% of the time, Pallas kernels for 0%

profile of v1, /device:TPU:0, one launch (start us, length us, event | category | flops | bytes accessed | tf_op | source)
XLA Modules:
  0.0 908.5 jit_solution(14349169153219333106)
XLA Ops:
  39.0 84.7 %all-gather.5.cloned.1.call-done = bf16[2560,2048]{1,0:T(8,128)(2,1)} async-done(((bf16[160,2048]{1,0:T(8,128)(2,1)}), bf16[2560,2048]{1,0:T(8,128)(2,1)}) %all-gather.5.cloned.1.call-update) | async-done | bytes 10485776 | tf_op jit(solution)/shard_map/all_gather | solution.py:122
  123.7 9.4 %fusion.66 = (bf16[2560,1024]{1,0:T(8,128)(2,1)}, bf16[2560,1024]{1,0:T(8,128)(2,1)}) fusion(bf16[2560,2048]{1,0:T(8,128)(2,1)} %all-gather.5.cloned.1.call-done), kind=kLoop, calls=%fused_computation.135 | loop fusion | bytes 20971520 | tf_op jit(solution)/shard_map/split | solution.py:121
  133.1 66.9 %while.26 = (s32[]{:T(128)}, f32[160,16,64]{0,2,1:T(8,128)}, f32[16,160]{1,0:T(8,128)S(1)}, bf16[2,1280,1024]{2,1,0:T(8,128)(2,1)}, s32[2,1280]{1,0:T(2,128)S(1)...) while((s32[]{:T(128)}, f32[160,16,64]{0,2,1:T(8,128)}, ...), condition=%wide.region_5.6_spmd.clone, body=%wide.region_3.5_spmd.clone.sunk | while | flops 859056768 | bytes 54739320 | solution.py:150
  143.2 10.0 %fusion.125 = (f32[16,160]{1,0:T(8,128)S(1)}, f32[16,1280,160]{1,2,0:T(8,128)}) fusion(pred[160,1280]{1,0:T(8,128)(4,1)S(1)} %broadcast_compare_fusion.4, bf16[1280,16,64]{0,2,1:T(8,128)(2,1)} %bitcast.211, bf16[160,16,64]{0,2,1:T(8,128)(2,1)S(1)} %get-tuple-element.522), kind=kOutput, calls=%fused_computation.3.clone.1 | convolution fusion | flops 429258240 | bytes 16271360 | tf_op jit(solution)/shard_map/while/body/eval_jaxpr/qhd,khd->hqk/dot_general | solution.py:136
  157.6 9.0 fusion.126
  176.6 9.8 %fusion.125 = (f32[16,160]{1,0:T(8,128)S(1)}, f32[16,1280,160]{1,2,0:T(8,128)}) fusion(pred[160,1280]{1,0:T(8,128)(4,1)S(1)} %broadcast_compare_fusion.4, bf16[1280,16,64]{0,2,1:T(8,128)(2,1)} %bitcast.211, bf16[160,16,64]{0,2,1:T(8,128)(2,1)S(1)} %get-tuple-element.522), kind=kOutput, calls=%fused_computation.3.clone.1 | convolution fusion | flops 429258240 | bytes 16271360 | tf_op jit(solution)/shard_map/while/body/eval_jaxpr/qhd,khd->hqk/dot_general | solution.py:136
  190.9 9.1 %fusion.126 = f32[160,16,64]{0,2,1:T(8,128)} fusion(bf16[1280,16,64]{0,2,1:T(8,128)(2,1)} %bitcast.212, f32[16,1280,160]{1,2,0:T(8,128)} %get-tuple-element.482, pred[160,1280]{1,0:T(8,128)(4,1)S(1)} %broadcast_compare_fusion.4, f32[160,16,64]{0,2,1:T(8,128)} %get-tuple-element.507, pred[]{:T(512)S(6)} %compare.6), kind=kOutput, calls=%fused_computation.10.clone.1 | convolution fusion | flops 429588480 | bytes 17244160 | tf_op jit(solution)/shard_map/while/body/eval_jaxpr/hqk,khd->qhd/dot_general | solution.py:142
  203.0 34.3 %all-gather.9.cloned.1.call-done = bf16[2560,1024]{1,0:T(8,128)(2,1)} async-done(((bf16[160,1024]{1,0:T(8,128)(2,1)}), bf16[2560,1024]{1,0:T(8,128)(2,1)}) %all-gather.9.cloned.1.call-update) | async-done | bytes 5242896 | tf_op jit(solution)/shard_map/all_gather | solution.py:195
  237.2 132.6 %while.27 = (s32[]{:T(128)}, f32[160,16,64]{0,2,1:T(8,128)}, bf16[2,1280,2048]{2,1,0:T(8,128)(2,1)}, bf16[2,1280,1024]{2,1,0:T(8,128)(2,1)}, s32[2,1280]{1,0:T(2...) while((s32[]{:T(128)}, f32[160,16,64]{0,2,1:T(8,128)}, ...), condition=%wide.region_9.10_spmd.clone, body=%wide.region_8.9_spmd.clone.sunk | while | flops 2137170048 | bytes 155306960 | solution.py:236
  247.3 8.3 fusion.137
  260.2 9.9 %fusion.138 = bf16[16,160,1280]{2,1,0:T(8,128)(2,1)S(1)} fusion(f32[16,1280,160]{1,2,0:T(8,128)} %fusion.137, bf16[1280,16,64]{0,2,1:T(8,128)(2,1)} %bitcast.213, bf16[160,16,64]{0,2,1:T(8,128)(2,1)} %get-tuple-element.557, f32[16,160]{1,0:T(8,128)S(1)} %bitcast.223, pred[160,1280]{1,0:T(8,128)(4,1)S(1)} %broadcast_compare_fusion.5), kind=kOutput, calls=%fused_computation.20.clone.1 | convolution fusion | flops 435814400 | bytes 22824960 | tf_op jit(solution)/shard_map/while/body/eval_jaxpr/qhd,khd->hqk/dot_general | solution.py:211
  273.0 7.2 fusion.140
  282.9 7.9 copy.122
  296.4 6.9 fusion.139
  313.2 8.3 fusion.137
  326.1 9.9 %fusion.138 = bf16[16,160,1280]{2,1,0:T(8,128)(2,1)S(1)} fusion(f32[16,1280,160]{1,2,0:T(8,128)} %fusion.137, bf16[1280,16,64]{0,2,1:T(8,128)(2,1)} %bitcast.213, bf16[160,16,64]{0,2,1:T(8,128)(2,1)} %get-tuple-element.557, f32[16,160]{1,0:T(8,128)S(1)} %bitcast.223, pred[160,1280]{1,0:T(8,128)(4,1)S(1)} %broadcast_compare_fusion.5), kind=kOutput, calls=%fused_computation.20.clone.1 | convolution fusion | flops 435814400 | bytes 22824960 | tf_op jit(solution)/shard_map/while/body/eval_jaxpr/qhd,khd->hqk/dot_general | solution.py:211
  338.9 7.2 fusion.140
  348.8 7.9 copy.122
  362.4 7.1 fusion.139
  386.7 101.4 %reduce-scatter.8.cloned.1.call-done = bf16[160,2048]{1,0:T(8,128)(2,1)} async-done(((bf16[2560,2048]{1,0:T(8,128)(2,1)}), bf16[160,2048]{1,0:T(8,128)(2,1)}) %reduce-scatter.8.cloned.1.call-update) | async-done | bytes 655376 | tf_op jit(solution)/shard_map/reduce_scatter | solution.py:246
  502.3 17.8 %all_gather.16 = bf16[320,1024]{1,0:T(8,128)(2,1)S(1)} all-gather(bf16[160,1024]{1,0:T(8,128)(2,1)S(1)} %copy-done.7), channel_id=1, replica_groups=mesh['dp'=16,'mlp'=2] {'mlp'}, dimensions={0}, use_global_device_ids=true | all-gather | bytes 983040 | tf_op jit(solution)/shard_map/all_gather | solution.py:163
  529.5 9.2 %all-gather = bf16[1,1,320,1024]{3,2,1,0:T(8,128)(2,1)S(1)} all-gather(bf16[1,1,160,1024]{3,2,1,0:T(8,128)(2,1)S(1)} %copy-done.9), channel_id=2, replica_groups=mesh['dp'=16,'mlp'=2] {'mlp'}, dimensions={2}, use_global_device_ids=true | all-gather | bytes 983040 | tf_op jit(solution)/shard_map/all_gather | solution.py:179
  538.6 6.7 fusion.69
  549.0 6.1 convolution_convert_fusion.2
  559.5 49.8 %reduce-scatter.12.cloned.1.call-done = bf16[1024,1536]{1,0:T(8,128)(2,1)} async-done(((bf16[1024,3072]{1,0:T(8,128)(2,1)}), bf16[1024,1536]{1,0:T(8,128)(2,1)}) %reduce-scatter.12.cloned.1.call-update) | async-done | bytes 3145744 | tf_op jit(solution)/shard_map/reduce_scatter | solution.py:269
  611.8 16.4 %reduce-scatter.6.cloned.1.call-done = bf16[160,1024]{1,0:T(8,128)(2,1)} async-done(((bf16[320,1024]{1,0:T(8,128)(2,1)}), bf16[160,1024]{1,0:T(8,128)(2,1)}) %reduce-scatter.6.cloned.1.call-update) | async-done | bytes 327696 | tf_op jit(solution)/shard_map/reduce_scatter | solution.py:167
  630.9 15.7 %reduce-scatter.10.cloned.1.call-done = bf16[160,1024]{1,0:T(8,128)(2,1)} async-done(((bf16[320,1024]{1,0:T(8,128)(2,1)}), bf16[160,1024]{1,0:T(8,128)(2,1)}) %reduce-scatter.10.cloned.1.call-update) | async-done | bytes 327696 | tf_op jit(solution)/shard_map/reduce_scatter | solution.py:185
  646.6 6.1 fusion.53
  652.6 6.9 all-reduce.6
  659.9 63.1 %all-reduce.4 = (bf16[512]{0:T(512)(128)(2,1)S(1)}, bf16[512]{0:T(512)(128)(2,1)S(1)}, bf16[1536]{0:T(1024)(128)(2,1)S(1)}, bf16[512]{0:T(512)(128)(2,1)S(1)}, bf16[2048]{0:T(1024)(128)(2,1)S(1)}) all-reduce(bf16[512]{0:T(512)(128)(2,1)S(1)} %dynamic-slice.2, ...), channel_id=1, replica_groups=mesh['dp'=16,'mlp'=2] {'dp'}, use_global_device_ids=true, to_apply=%region_16.17 | all-reduce | flops 5120 | bytes 20480 | tf_op jit(solution)/shard_map/psum | solution.py:293
  727.6 157.1 %all-reduce.9.cloned.1.call-done = (bf16[1024,1536]{1,0:T(8,128)(2,1)}, bf16[1024,512]{1,0:T(8,128)(2,1)}, bf16[1024,2048]{1,0:T(8,128)(2,1)}, bf16[2048,1024]{1,0:T(8,128)(2,1)}) async-done(((bf16[1024,1536]{1,0:T(8,128)(2,1)}, bf16[1024,512]{1,0:T(8,128)(2,1)}, bf16[1024,2048]{1,0:T(8,128)(2,1)}, bf16[2048,1024]{1,0:T(8,128)(2,1)}), (bf16[1024,1536]{1,0:T(8,128)(2,1)}, bf16[1024,512]{1,0:T(8,128)(2,1)}, ...) | async-done | bytes 12582928 | tf_op jit(solution)/shard_map/psum | solution.py:289
  884.7 6.8 convert_element_type.175
  (208 shorter events, 181.1 us)
Async XLA Ops:
  7.2 192.8 %copy-start = (bf16[1024,1024]{1,0:T(8,128)(2,1)S(1)}, bf16[1024,1024]{1,0:T(8,128)(2,1)}, u32[]{:S(2)}) copy-start(bf16[1024,1024]{1,0:T(8,128)(2,1)} %param.23) | copy-start | bytes 6291460
  7.2 116.5 %all-gather.5.cloned.1.call-start = ((), (), s32[]{:S(2)}) async-start(), calls=%async_computation.5 | async-start | bytes 11141120 | tf_op jit(solution)/shard_map/all_gather | solution.py:122
  11.6 4.1 copy-start.6
  19.5 5.3 copy-start.15
  33.3 169.6 %all-gather.7.cloned.1.call-start = ((), (), s32[]{:S(2)}) async-start(), calls=%async_computation.7 | async-start | bytes 5570560 | tf_op jit(solution)/shard_map/all_gather | solution.py:194
  34.1 203.2 %all-gather.9.cloned.1.call-start = ((), (), s32[]{:S(2)}) async-start(), calls=%async_computation.8 | async-start | bytes 5570560 | tf_op jit(solution)/shard_map/all_gather | solution.py:195
  34.8 453.4 %reduce-scatter.8.cloned.1.call-start = ((), (), s32[]{:S(2)}) async-start(), calls=%async_computation.9 | async-start | bytes 11141120 | tf_op jit(solution)/shard_map/reduce_scatter | solution.py:246
  133.1 66.9 %copy-start.8 = (bf16[1,1,160,1024]{3,2,1,0:T(8,128)(2,1)S(1)}, bf16[1,1,160,1024]{3,2,1,0:T(8,128)(2,1)}, u32[]{:S(2)}) copy-start(bf16[1,1,160,1024]{3,2,1,0:T(8,128)(2,1)} %param.29) | copy-start | bytes 983044
  369.9 5.5 copy-start.2
  369.9 189.5 %reduce-scatter.14.cloned.1.call-start = ((), (), s32[]{:S(2)}) async-start(), calls=%async_computation.12 | async-start | bytes 3145728 | tf_op jit(solution)/shard_map/reduce_scatter | solution.py:272
  373.9 4.0 copy-start.16
  373.9 235.3 %reduce-scatter.12.cloned.1.call-start = ((), (), s32[]{:S(2)}) async-start(), calls=%async_computation.11 | async-start | bytes 9437184 | tf_op jit(solution)/shard_map/reduce_scatter | solution.py:269
  377.9 6.9 copy-start.14
  502.3 17.9 %copy-start.33 = (f32[2048]{0:T(1024)S(1)}, f32[2048]{0:T(1024)}, u32[]{:S(2)}) copy-start(f32[2048]{0:T(1024)} %param.26) | copy-start | bytes 24580
  502.3 125.9 %reduce-scatter.6.cloned.1.call-start = ((), (), s32[]{:S(2)}) async-start(), calls=%async_computation.6 | async-start | bytes 983040 | tf_op jit(solution)/shard_map/reduce_scatter | solution.py:167
  520.2 5.7 copy-start.19
  520.2 6.8 copy-start.31
  529.4 117.2 %reduce-scatter.10.cloned.1.call-start = ((), (), s32[]{:S(2)}) async-start(), calls=%async_computation.10 | async-start | bytes 983040 | tf_op jit(solution)/shard_map/reduce_scatter | solution.py:185
  538.6 6.7 copy-start.20
  538.6 7.8 copy-start.32
  548.9 335.8 %all-reduce.9.cloned.1.call-start = ((), (), s32[]{:S(2)}) async-start(), calls=%async_computation.13 | async-start | bytes 25165824 | tf_op jit(solution)/shard_map/psum | solution.py:289
  548.9 6.1 copy-start.21
  549.0 6.1 copy-start.36
  609.3 18.9 %copy-start.5 = (bf16[1,1,160,1024]{3,2,1,0:T(8,128)(2,1)S(1)}, bf16[1,1,160,1024]{3,2,1,0:T(8,128)(2,1)}, u32[]{:S(2)}) copy-start(bf16[1,1,160,1024]{3,2,1,0:T(8,128)(2,1)} %param.17) | copy-start | bytes 983044
  609.3 18.9 %copy-start.22 = (f32[1024]{0:T(1024)S(1)}, f32[1024]{0:T(1024)}, u32[]{:S(2)}) copy-start(f32[1024]{0:T(1024)} %param.28) | copy-start | bytes 12292
  609.3 18.9 %copy-start.23 = (f32[1024]{0:T(1024)S(1)}, f32[1024]{0:T(1024)}, u32[]{:S(2)}) copy-start(f32[1024]{0:T(1024)} %param.24) | copy-start | bytes 12292
  609.3 37.2 %copy-start.25 = (f32[160]{0:T(256)S(1)}, f32[160]{0:T(256)}, u32[]{:S(2)}) copy-start(f32[160]{0:T(256)} %copy-done.24) | copy-start | bytes 1924
  609.4 37.2 %copy-start.26 = (f32[1024]{0:T(1024)S(1)}, f32[1024]{0:T(1024)}, u32[]{:S(2)}) copy-start(f32[1024]{0:T(1024)} %param.19) | copy-start | bytes 12292
  609.4 37.2 %copy-start.28 = (f32[160]{0:T(256)S(1)}, f32[160]{0:T(256)}, u32[]{:S(2)}) copy-start(f32[160]{0:T(256)} %copy-done.27) | copy-start | bytes 1924
  724.2 176.9 %copy-start.29 = (f32[512]{0:T(512)}, f32[512]{0:T(512)S(1)}, u32[]{:S(2)}) copy-start(f32[512]{0:T(512)S(1)} %convert_element_type.173) | copy-start | bytes 6148
  884.7 6.8 copy-start.10
  891.5 4.4 copy-start.11
  (17 other events, 34.6 us)
Sparse Core Ops, SparseCore 0:
  33.4 90.2 all-gather.4
  126.0 53.9 all-gather.6
  182.9 54.3 all-gather.8
  370.0 118.0 reduce-scatter.7
  490.8 38.5 reduce-scatter.13
  532.1 77.1 reduce-scatter.11
  612.1 16.0 reduce-scatter.5
  630.5 16.0 reduce-scatter.9
  651.7 232.9 all-reduce.8
